TPU v7x, 32 devices: a whole 2x2x4 slice. The times are simulated.
32 devices in a mesh: row: 8 (over y, x, core), col: 4 (over z).
Axes of the slice: x: 2, y: 2, z: 4, core: 2. Of those that a mesh axis runs over, the one named last changes fastest.
Arguments:
- samples: float32 [32768, 32], P(('row', 'col')), may hold values from -3 to 3
- sample_logw: float32 [32768], P(('row', 'col')), may hold values from -8 to 8
- references: float32 [65536, 32], P(('row', 'col')), may hold values from -3 to 3
- reference_logw: float32 [65536], P(('row', 'col')), may hold values from -8 to 8
- dual_start: float32 [8, 4096], P('row'), may hold values from -3 to 3
- kept_tiles: int32 [8, 4, 32], P('row', 'col'), may hold values from 0 to 255, as said below
- tile_counts: int32 [8, 4], P('row', 'col'), may hold values from 4 to 32, as said below
Outputs:
- row_duals: float32 [8, 4096], P('row')
- col_duals: float32 [4, 16384], P('col')
Inputs may be any that keep to these rules, and one draw needn't show every extreme that they name: `kept_tiles`: on device (i, j) the first tile_counts[i, j] entries are distinct tiles r * 32 + c of its 8 by 32 grid; later entries are tiles of that grid and unused. Every block of every sample group and of every reference group lies in some used tile. `tile_counts`: 32 on at least one device.
All inputs are finite; a program needn't handle non-finite values.
Results may differ from a plain program's by a relative error of at most 0.0003.
Values sent between devices are 32-bit elements; how exact they have to be, the bound alone decides.
No kernel may reach another device: no remote copies, remote signals or barrier semaphores. Data moves between devices by JAX's collectives and lax.ppermute only.
A program may use at most 64 MiB of HBM per device.

v0:
```python
import jax
import jax.numpy as jnp
from jax import lax
from jax.sharding import PartitionSpec as P

TILE = 512
ITERS = 3


lowest = -1e30
epsilon = 0.1


def from_partner(shard, axis, distance):
    return lax.ppermute(shard, axis, [(i, i ^ 1 << distance) for i in range(lax.axis_size(axis))])


def merged_2(value, axis, join):
    pieces = jax.tree.map(lambda part: lax.all_gather(part, axis), value)
    head = jax.tree.map(lambda part: part[0], pieces)
    tail = jax.tree.map(lambda part: part[1:], pieces)
    total, _ = lax.scan(lambda total, piece: (join(total, piece), None), head, tail)
    return total


def combine(left, right):
    peak = jnp.maximum(left[0], right[0])
    return (peak, left[1] * jnp.exp(left[0] - peak) + right[1] * jnp.exp(right[0] - peak))


def tile_cost(row_points, row_norms, col_points, col_norms):
    inner = jnp.dot(
        row_points,
        col_points.T,
        precision=lax.Precision.HIGHEST,
        preferred_element_type=jnp.float32,
    )
    return row_norms[:, None] + col_norms[None, :] - 2.0 * inner


def per_device(
    samples, sample_logw, references, reference_logw, dual_start, kept_tiles, tile_counts
):
    sample_group, sample_weights = (
        lax.all_gather(samples, "col", axis=0, tiled=True),
        lax.all_gather(sample_logw, "col", axis=0, tiled=True),
    )
    reference_group, reference_weights = (
        lax.all_gather(references, "row", axis=0, tiled=True),
        lax.all_gather(reference_logw, "row", axis=0, tiled=True),
    )
    block = TILE
    slots = kept_tiles.shape[2]
    col_blocks = reference_group.shape[0] // block
    sample_norms = jnp.sum(sample_group * sample_group, axis=1)
    reference_norms = jnp.sum(reference_group * reference_group, axis=1)
    own_tiles = kept_tiles[0, 0]
    own_count = tile_counts[0]
    partner_group, partner_weights, partner_tiles, partner_count = from_partner(
        (sample_group, sample_weights, own_tiles, own_count), "row", 0
    )
    is_low = lax.axis_index("row") % 2 == 0
    low_tiles = jnp.where(is_low, own_tiles, partner_tiles)
    high_tiles = jnp.where(is_low, partner_tiles, own_tiles)
    low_count = jnp.where(is_low, own_count[0], partner_count[0])
    high_count = jnp.where(is_low, partner_count[0], own_count[0])
    half = (low_count + high_count + 1) // 2
    first = jnp.where(is_low, 0, half)
    work = jnp.where(is_low, half, low_count + high_count - half)

    def locate(step):
        position = first + step
        from_low = position < low_count
        tile = jnp.where(
            from_low,
            low_tiles[jnp.minimum(position, slots - 1)],
            high_tiles[jnp.clip(position - low_count, 0, slots - 1)],
        )
        source = jnp.where(from_low == is_low, 0, 1).astype(jnp.int32)
        return (source, tile)

    group_stack = jnp.stack([sample_group, partner_group])
    weight_stack = jnp.stack([sample_weights, partner_weights])
    norm_stack = jnp.stack([sample_norms, jnp.sum(partner_group * partner_group, axis=1)])
    sources = group_stack.shape[0]
    row_width = group_stack.shape[1]
    col_width = reference_group.shape[0]

    def cost_at(step):
        source, tile = locate(step)
        row_start = tile // col_blocks * block
        col_start = tile % col_blocks * block
        row_points = lax.dynamic_slice(
            group_stack, (source, row_start, 0), (1, block, group_stack.shape[2])
        )[0]
        row_norms = lax.dynamic_slice(norm_stack, (source, row_start), (1, block))[0]
        col_points = lax.dynamic_slice_in_dim(reference_group, col_start, block, 0)
        col_norms = lax.dynamic_slice_in_dim(reference_norms, col_start, block, 0)
        return (
            source,
            row_start,
            col_start,
            tile_cost(row_points, row_norms, col_points, col_norms),
        )

    dual_row = dual_start[0]
    dual_col = jnp.zeros((col_width,), jnp.float32)
    for turn in range(ITERS):
        dual_stack = jnp.stack([dual_row, from_partner(dual_row, "row", 0)])

        def column_visit(step, carry):
            source, row_start, col_start, cost = cost_at(step)
            weights = lax.dynamic_slice(weight_stack, (source, row_start), (1, block))[0]
            duals = lax.dynamic_slice(dual_stack, (source, row_start), (1, block))[0]
            score = weights[:, None] + (duals[:, None] - cost) / epsilon
            peak = jnp.max(score, axis=0)
            total = jnp.sum(jnp.exp(score - peak[None, :]), axis=0)
            before = (
                lax.dynamic_slice_in_dim(carry[0], col_start, block, 0),
                lax.dynamic_slice_in_dim(carry[1], col_start, block, 0),
            )
            merged = combine(before, (peak, total))
            return (
                lax.dynamic_update_slice_in_dim(carry[0], merged[0], col_start, 0),
                lax.dynamic_update_slice_in_dim(carry[1], merged[1], col_start, 0),
            )

        column_start_state = (
            jnp.full((col_width,), lowest, jnp.float32),
            jnp.zeros((col_width,), jnp.float32),
        )
        col_peak, col_total = merged_2(
            lax.fori_loop(0, work, column_visit, column_start_state), "row", combine
        )
        dual_col = -epsilon * (col_peak + jnp.log(col_total))

        def row_visit(step, carry):
            source, row_start, col_start, cost = cost_at(step)
            weights = lax.dynamic_slice_in_dim(reference_weights, col_start, block, 0)
            duals = lax.dynamic_slice_in_dim(dual_col, col_start, block, 0)
            score = weights[None, :] + (duals[None, :] - cost) / epsilon
            peak = jnp.max(score, axis=1)
            total = jnp.sum(jnp.exp(score - peak[:, None]), axis=1)
            before = (
                lax.dynamic_slice(carry[0], (source, row_start), (1, block))[0],
                lax.dynamic_slice(carry[1], (source, row_start), (1, block))[0],
            )
            merged = combine(before, (peak, total))
            return (
                lax.dynamic_update_slice(carry[0], merged[0][None], (source, row_start)),
                lax.dynamic_update_slice(carry[1], merged[1][None], (source, row_start)),
            )

        start_state = (
            jnp.full((sources, row_width), lowest, jnp.float32),
            jnp.zeros((sources, row_width), jnp.float32),
        )
        row_peaks, row_sums = lax.fori_loop(0, work, row_visit, start_state)
        returned = from_partner((row_peaks[1], row_sums[1]), "row", 0)
        row_peak, row_total = merged_2(
            combine((row_peaks[0], row_sums[0]), returned), "col", combine
        )
        dual_row = -epsilon * (row_peak + jnp.log(row_total))
    return (dual_row[None], dual_col[None])


def solution(mesh):
    return jax.shard_map(
        per_device,
        mesh=mesh,
        in_specs=(
            P(("row", "col"), None),
            P(("row", "col")),
            P(("row", "col"), None),
            P(("row", "col")),
            P("row", None),
            P("row", "col", None),
            P("row", "col"),
        ),
        out_specs=(P("row", None), P("col", None)),
        check_vma=False,
    )
```

profile of v0, /device:TPU:0, one launch (start us, length us, event | category | flops | bytes accessed | tf_op | source)
XLA Modules:
  0.0 855.7 jit_solution(13692131083154798649)
XLA Ops:
  10.2 15.0 %all_gather.85 = f32[4096]{0:T(1024)S(1)} all-gather(f32[1024]{0:T(1024)} %param.32), channel_id=1, replica_groups=mesh['row'=8,'col'=4] {'col'}, dimensions={0}, use_global_device_ids=true | all-gather | bytes 20480 | tf_op jit(solution)/shard_map/all_gather | solution.py:46
  25.7 16.0 %all_gather.86 = f32[4096,32]{0,1:T(8,128)S(1)} all-gather(f32[1024,32]{0,1:T(8,128)} %param.31), channel_id=1, replica_groups=mesh['row'=8,'col'=4] {'col'}, dimensions={0}, use_global_device_ids=true | all-gather | bytes 655360 | tf_op jit(solution)/shard_map/all_gather | solution.py:45
  42.3 9.6 %all_gather.84 = f32[16384]{0:T(1024)S(1)} all-gather(f32[2048]{0:T(1024)} %param.34), channel_id=1, replica_groups=mesh['row'=8,'col'=4] {'row'}, dimensions={0}, use_global_device_ids=true | all-gather | bytes 73728 | tf_op jit(solution)/shard_map/all_gather | solution.py:50
  54.8 2.7 copy.12
  57.6 9.5 %all-gather.14.cloned.1.call-done = f32[16384,32]{1,0:T(8,128)} async-done(((f32[2048,32]{1,0:T(8,128)}), f32[16384,32]{1,0:T(8,128)}) %all-gather.14.cloned.1.call-update) | async-done | bytes 2097168 | tf_op jit(solution)/shard_map/all_gather | solution.py:49
  67.1 4.6 multiply_reduce_fusion
  71.8 101.8 %while.156 = (s32[]{:T(128)}, f32[16384]{0:T(1024)S(1)}, f32[16384]{0:T(1024)S(1)}, s32[]{:T(128)}, s32[]{:T(128)}, /*index=5*/s32[]{:T(128)}, s32[32]{0:T(128)S...) while((s32[]{:T(128)}, f32[16384]{0:T(1024)S(1)}, ...), condition=%wide.region_6.7_spmd, body=%wide.region_3.6_spmd.sunk | while | flops 103024680 | bytes 2665136 | solution.py:133
  173.6 8.5 all-gather.1
  182.1 10.2 %all-gather = f32[131072]{0:T(1024)S(1)} all-gather(f32[16384]{0:T(1024)S(1)} %get-tuple-element.1322), channel_id=2, replica_groups=mesh['row'=8,'col'=4] {'row'}, dimensions={0}, use_global_device_ids=true | all-gather | bytes 589824 | tf_op jit(solution)/shard_map/all_gather | solution.py:19
  194.3 108.5 %while.158 = (s32[]{:T(128)}, f32[2,4096]{1,0:T(2,128)S(1)}, f32[2,4096]{1,0:T(2,128)S(1)}, s32[]{:T(128)}, s32[]{:T(128)}, /*index=5*/s32[]{:T(128)}, pred[]{:T...) while((s32[]{:T(128)}, f32[2,4096]{1,0:T(2,128)S(1)}, ...), condition=%wide.region_12.13_spmd, body=%wide.region_9.12_spmd.sunk | while | flops 103024680 | bytes 2673340 | solution.py:158
  304.5 13.1 %all-gather.3 = f32[16384]{0:T(1024)S(1)} all-gather(f32[4096]{0:T(1024)S(1)} %get-tuple-element.1692), channel_id=5, replica_groups=mesh['row'=8,'col'=4] {'col'}, dimensions={0}, use_global_device_ids=true | all-gather | bytes 81920 | tf_op jit(solution)/shard_map/all_gather | solution.py:19
  317.6 13.1 %all-gather.2 = f32[16384]{0:T(1024)S(1)} all-gather(f32[4096]{0:T(1024)S(1)} %get-tuple-element.1693), channel_id=4, replica_groups=mesh['row'=8,'col'=4] {'col'}, dimensions={0}, use_global_device_ids=true | all-gather | bytes 81920 | tf_op jit(solution)/shard_map/all_gather | solution.py:19
  332.4 99.1 %while.160 = (s32[]{:T(128)}, f32[16384]{0:T(1024)S(1)}, f32[16384]{0:T(1024)S(1)}, s32[]{:T(128)}, s32[]{:T(128)}, /*index=5*/s32[]{:T(128)}, s32[32]{0:T(128)S...) while((s32[]{:T(128)}, f32[16384]{0:T(1024)S(1)}, ...), condition=%wide.region_18.19_spmd, body=%wide.region_15.18_spmd.sunk | while | flops 103024680 | bytes 2665136 | solution.py:133
  431.6 8.5 all-gather.5
  440.1 10.2 %all-gather.4 = f32[131072]{0:T(1024)S(1)} all-gather(f32[16384]{0:T(1024)S(1)} %get-tuple-element.1330), channel_id=6, replica_groups=mesh['row'=8,'col'=4] {'row'}, dimensions={0}, use_global_device_ids=true | all-gather | bytes 589824 | tf_op jit(solution)/shard_map/all_gather | solution.py:19
  452.3 109.1 %while.162 = (s32[]{:T(128)}, f32[2,4096]{1,0:T(2,128)S(1)}, f32[2,4096]{1,0:T(2,128)S(1)}, s32[]{:T(128)}, s32[]{:T(128)}, /*index=5*/s32[]{:T(128)}, pred[]{:T...) while((s32[]{:T(128)}, f32[2,4096]{1,0:T(2,128)S(1)}, ...), condition=%wide.region_24.25_spmd, body=%wide.region_21.24_spmd.sunk | while | flops 103024680 | bytes 2673340 | solution.py:158
  563.0 13.1 %all-gather.7 = f32[16384]{0:T(1024)S(1)} all-gather(f32[4096]{0:T(1024)S(1)} %get-tuple-element.1690), channel_id=9, replica_groups=mesh['row'=8,'col'=4] {'col'}, dimensions={0}, use_global_device_ids=true | all-gather | bytes 81920 | tf_op jit(solution)/shard_map/all_gather | solution.py:19
  576.2 13.1 %all-gather.6 = f32[16384]{0:T(1024)S(1)} all-gather(f32[4096]{0:T(1024)S(1)} %get-tuple-element.1691), channel_id=8, replica_groups=mesh['row'=8,'col'=4] {'col'}, dimensions={0}, use_global_device_ids=true | all-gather | bytes 81920 | tf_op jit(solution)/shard_map/all_gather | solution.py:19
  591.0 99.0 %while.164 = (s32[]{:T(128)}, f32[16384]{0:T(1024)S(1)}, f32[16384]{0:T(1024)S(1)}, s32[]{:T(128)}, s32[]{:T(128)}, /*index=5*/s32[]{:T(128)}, s32[32]{0:T(128)S...) while((s32[]{:T(128)}, f32[16384]{0:T(1024)S(1)}, ...), condition=%wide.region_30.31_spmd, body=%wide.region_27.30_spmd.sunk | while | flops 103024680 | bytes 2665136 | solution.py:133
  689.9 8.5 all-gather.9
  698.5 10.2 %all-gather.8 = f32[131072]{0:T(1024)S(1)} all-gather(f32[16384]{0:T(1024)S(1)} %get-tuple-element.1338), channel_id=10, replica_groups=mesh['row'=8,'col'=4] {'row'}, dimensions={0}, use_global_device_ids=true | all-gather | bytes 589824 | tf_op jit(solution)/shard_map/all_gather | solution.py:19
  710.6 109.3 %while.166 = (s32[]{:T(128)}, f32[2,4096]{1,0:T(2,128)S(1)}, f32[2,4096]{1,0:T(2,128)S(1)}, s32[]{:T(128)}, s32[]{:T(128)}, /*index=5*/s32[]{:T(128)}, pred[]{:T...) while((s32[]{:T(128)}, f32[2,4096]{1,0:T(2,128)S(1)}, ...), condition=%wide.region_36.37_spmd, body=%wide.region_33.36_spmd.sunk | while | flops 103024680 | bytes 2673340 | solution.py:158
  821.6 13.1 %all-gather.11 = f32[16384]{0:T(1024)S(1)} all-gather(f32[4096]{0:T(1024)S(1)} %get-tuple-element.1688), channel_id=13, replica_groups=mesh['row'=8,'col'=4] {'col'}, dimensions={0}, use_global_device_ids=true | all-gather | bytes 81920 | tf_op jit(solution)/shard_map/all_gather | solution.py:19
  834.8 13.1 %all-gather.10 = f32[16384]{0:T(1024)S(1)} all-gather(f32[4096]{0:T(1024)S(1)} %get-tuple-element.1689), channel_id=12, replica_groups=mesh['row'=8,'col'=4] {'col'}, dimensions={0}, use_global_device_ids=true | all-gather | bytes 81920 | tf_op jit(solution)/shard_map/all_gather | solution.py:19
  (1248 shorter events, 501.6 us)
Async XLA Ops:
  7.2 60.0 %all-gather.14.cloned.1.call-start = ((), (), s32[]{:S(2)}) async-start(), calls=%async_computation | async-start | bytes 9437184 | tf_op jit(solution)/shard_map/all_gather | solution.py:49
  9.6 43.7 %collective-permute-start.1 = (s32[32]{0:T(128)}, s32[32]{0:T(128)S(1)}, u32[]{:S(2)}, u32[]{:S(2)}) collective-permute-start(s32[32]{0:T(128)} %bitcast.258), channel_id=1, source_target_pairs={{0,4},{4,0},{8,12},{12,8},{16,20},{20,16},{24,28},{28,24},{1,5},{5... | collective-permute-start | bytes 392 | tf_op jit(solution)/shard_map/ppermute | solution.py:15
  10.1 41.9 %collective-permute-start = (s32[1]{0:T(128)}, s32[1]{0:T(128)}, u32[]{:S(2)}, u32[]{:S(2)}) collective-permute-start(s32[1]{0:T(128)} %bitcast.49), channel_id=1, source_target_pairs={{0,4},{4,0},{8,12},{12,8},{16,20},{20,16},{24,28},{28,24},{1,5},{5... | collective-permute-start | bytes 20 | tf_op jit(solution)/shard_map/ppermute | solution.py:15
  25.2 29.5 %collective-permute-start.2 = (f32[4096]{0:T(1024)S(1)}, f32[4096]{0:T(1024)S(1)}, u32[]{:S(2)}, u32[]{:S(2)}) collective-permute-start(f32[4096]{0:T(1024)S(1)} %all_gather.85), channel_id=1, source_target_pairs={{0,4},{4,0},{8,12},{12,8},{16,20},{20,16},{24,28},{28,24},{1,5},{5... | collective-permute-start | bytes 49160 | tf_op jit(solution)/shard_map/ppermute | solution.py:15
  25.2 28.8 %collective-permute-start.3 = (f32[4096]{0:T(1024)}, f32[4096]{0:T(1024)S(1)}, u32[]{:S(2)}, u32[]{:S(2)}) collective-permute-start(f32[4096]{0:T(1024)} %bitcast.247), channel_id=1, source_target_pairs={{0,4},{4,0},{8,12},{12,8},{16,20},{20,16},{24,28},{28,24},{1,5},{5... | collective-permute-start | bytes 49160 | tf_op jit(solution)/shard_map/ppermute | solution.py:15
  41.6 13.1 %collective-permute-start.4 = (f32[4096,32]{0,1:T(8,128)S(1)}, f32[4096,32]{0,1:T(8,128)S(1)}, u32[]{:S(2)}, u32[]{:S(2)}) collective-permute-start(f32[4096,32]{0,1:T(8,128)S(1)} %all_gather.86), channel_id=1, source_target_pairs={{0,4},{4,0},{8,12},{12,8},{16,20},{20,16},{24,28},{28,24},{1,5},{5... | collective-permute-start | bytes 1572872 | tf_op jit(solution)/shard_map/ppermute | solution.py:15
  302.9 1.2 collective-permute-start.5
  303.3 1.2 collective-permute-start.6
  331.1 1.2 collective-permute-start.7
  561.4 1.2 collective-permute-start.9
  561.7 1.2 collective-permute-start.8
  589.6 1.2 collective-permute-start.10
  819.9 28.9 %copy-start = (f32[16384]{0:T(1024)}, f32[16384]{0:T(1024)S(1)}, u32[]{:S(2)}) copy-start(f32[16384]{0:T(1024)S(1)} %get-tuple-element.3150) | copy-start | bytes 196612
  820.0 1.2 collective-permute-start.12
  820.4 1.2 collective-permute-start.11
Sparse Core Ops, SparseCore 0:
  9.9 57.2 all-gather.13
where the time goes:
time: 859 us; the launch traced here: 856 us
  matrix products  242 us (28%)
  local copies, waits for them, and re-layouts  206 us (24%)
  blocking collectives  175 us (20%)
  loops' own time  151 us (18%)
  other arithmetic  47.1 us (5%)
  between operations  16.5 us (2%)
  waiting for transfers between devices  14.7 us (2%)
    dot_general x108, matrix products, tile_cost(): jnp.dot(row_points, col_points.T, precision=lax.Precision.HIGHEST, prefer...  242 us
    all_gather x12, blocking collectives, merged_2(): pieces = jax.tree.map(lambda part: lax.all_gather(part, axis), value)  135 us
    another operation x3, loops' own time, per_device(): row_peaks, row_sums = lax.fori_loop(0, work, row_visit, start_state)  77.6 us
    another operation x3, loops' own time, per_device(): lax.fori_loop(0, work, column_visit, column_start_state)  72.6 us
    dynamic_slice x108, local copies, waits for them, and re-layouts, locate(): low_tiles[jnp.minimum(position, slots - 1)]  68.2 us
    dynamic_slice x108, local copies, waits for them, and re-layouts, locate(): high_tiles[jnp.clip(position - low_count, 0, slots - 1)]  68 us
  transfers between devices with their start and end apart: 14, of which 9 were waited for; matrix products, arithmetic and copies ran while one was open for 1% of the time, Pallas kernels for 0%

commit v1 on v0

v1 whole, which is shorter than its diff:
```python
import functools
import math

import jax
import jax.numpy as jnp
from jax import lax
from jax.experimental import pallas as pl
from jax.experimental.pallas import tpu as pltpu
from jax.sharding import PartitionSpec as P

TILE = 512
ITERS = 3
LANES = 128
BIAS = 16

lowest = -1e30
epsilon = 0.1
log2e = math.log2(math.e)
ln2 = math.log(2.0)

VM = pl.BlockSpec(memory_space=pltpu.VMEM)
SM = pl.BlockSpec(memory_space=pltpu.SMEM)
PARAMS = pltpu.CompilerParams(vmem_limit_bytes=24 * 1024 * 1024)


def swap(value, axis, distance):
    pairs = [(i, i ^ distance) for i in range(lax.axis_size(axis))]
    return jax.tree.map(lambda part: lax.ppermute(part, axis, pairs), value)


def pack_kernel(xt_ref, wx_ref, yt_ref, wy_ref, x_ref, keep_ref, *send_refs):
    dim = xt_ref.shape[0]
    chunks = TILE // LANES

    def put(out, b, points_ref, weights_ref, block):
        for j in range(chunks):
            start = pl.multiple_of(block * TILE + j * LANES, LANES)
            out[b, j * dim : (j + 1) * dim, :] = points_ref[:, pl.ds(start, LANES)]
        out[b, chunks * dim : chunks * dim + chunks, :] = weights_ref[pl.ds(block * chunks, chunks), :]

    for b in range(x_ref.shape[0]):
        put(x_ref, b, xt_ref, wx_ref, b)
    if send_refs:
        parity = lax.rem(lax.axis_index("row"), 2)
        for b in range(keep_ref.shape[0]):
            put(keep_ref, b, yt_ref, wy_ref, 2 * b + parity)
            put(send_refs[0], b, yt_ref, wy_ref, 2 * b + 1 - parity)
    else:
        for b in range(keep_ref.shape[0]):
            put(keep_ref, b, yt_ref, wy_ref, b)


def prepare(own_x, partner_x, own_y, partner_y, dual_own, dual_partner, tiles_own, tiles_partner, sizes):
    row_blocks, col_blocks, dim = sizes
    n_x, n_y = len(own_x), len(own_y)
    both = len(partner_y) > 0
    slots = tiles_own.shape[0] - 1
    per_x = own_x[0].shape[0]
    per_y = own_y[0].shape[0] * (2 if both else 1)
    half_cols = col_blocks // 2
    all_rows = 2 * row_blocks
    chunks = TILE // LANES

    def kernel(*refs):
        refs = list(refs)

        def take(n):
            out = refs[:n]
            del refs[:n]
            return out

        xs, pxs, ys, pys = take(n_x), take(n_x), take(n_y), take(len(partner_y))
        d_own, d_partner, t_own, t_partner = take(4)
        xp, yp, u0, wx, wy, nx, ny, m_list, n_list, count = take(10)
        row, col = lax.axis_index("row"), lax.axis_index("col")
        parity = lax.rem(row, 2)
        pair = lax.div(row, 2)

        def load(ref, b):
            points = jnp.concatenate([ref[b, j * dim : (j + 1) * dim, :] for j in range(chunks)], axis=1)
            base = chunks * dim
            weights = jnp.concatenate([ref[b, base + j : base + j + 1, :] for j in range(chunks)], axis=1)
            return points, weights

        def split(out, index, points):
            high = points.astype(jnp.bfloat16)
            low = (points - high.astype(jnp.float32)).astype(jnp.bfloat16)
            out[index, 0:dim, :] = high
            out[index, dim : 2 * dim, :] = low

        for group, (sources, duals) in enumerate(((xs, d_own), (pxs, d_partner))):
            side = parity if group == 0 else 1 - parity
            for d in range(n_x):
                for b in range(per_x):
                    local = (col ^ d) * per_x + b
                    index = side * row_blocks + local
                    points, weights = load(sources[d], b)
                    norm = jnp.sum(points * points, axis=0, keepdims=True)
                    split(xp, index, points * (2.0 * log2e / epsilon))
                    start = pl.multiple_of(local * TILE, TILE)
                    dual = duals[0:1, pl.ds(start, TILE)]
                    u0[pl.ds(index, 1), :] = log2e * weights + (dual - norm) * (log2e / epsilon)
                    wx[pl.ds(index, 1), :] = log2e * weights
                    nx[pl.ds(index, 1), :] = norm
        for d in range(n_y):
            place = pair ^ d
            for from_partner in range(2 if both else 1):
                source = (ys, pys)[from_partner][d]
                here = source.shape[0]
                for b in range(here):
                    index = place * per_y + b
                    if both:
                        index = index + (parity if from_partner == 0 else 1 - parity) * here
                    points, weights = load(source, b)
                    norm = jnp.sum(points * points, axis=0, keepdims=True)
                    split(yp, index, points)
                    wy[pl.ds(index, 1), :] = log2e * weights
                    ny[pl.ds(index, 1), :] = norm

        def collect(ref, side, filled):
            def visit(k, filled):
                tile = ref[k]
                r, c = lax.div(tile, col_blocks), lax.rem(tile, col_blocks)

                @pl.when(lax.rem(c, 2) == parity)
                def _():
                    m_list[filled] = side * row_blocks + r
                    n_list[filled] = lax.div(c, 2)

                return filled + (lax.rem(c, 2) == parity).astype(jnp.int32)

            return lax.fori_loop(0, ref[slots], visit, filled)

        filled = collect(t_own, parity, jnp.int32(0))
        filled = collect(t_partner, 1 - parity, filled)
        count[0] = filled
        m_list[filled] = 0
        n_list[filled] = 0
        m_list[filled + 1] = 0
        n_list[filled + 1] = 0

    f32, bf16, i32 = jnp.float32, jnp.bfloat16, jnp.int32
    shape = jax.ShapeDtypeStruct
    rows, cols = (all_rows, TILE), (half_cols, TILE)
    capacity = 2 * slots + 2
    return pl.pallas_call(
        kernel,
        out_shape=(
            shape((all_rows, 2 * dim, TILE), bf16),
            shape((half_cols, 2 * dim, TILE), bf16),
            shape(rows, f32),
            shape(rows, f32),
            shape(cols, f32),
            shape(rows, f32),
            shape(cols, f32),
            shape((capacity,), i32),
            shape((capacity,), i32),
            shape((1,), i32),
        ),
        in_specs=[VM] * (2 * n_x + n_y + len(partner_y) + 2) + [SM] * 2,
        out_specs=(VM,) * 7 + (SM,) * 3,
        compiler_params=PARAMS,
        name="prepare",
    )(*own_x, *partner_x, *own_y, *partner_y, dual_own, dual_partner, tiles_own, tiles_partner)


def log_sum(parts):
    if len(parts) == 1:
        return parts[0]
    peak = functools.reduce(jnp.maximum, parts)
    total = functools.reduce(jnp.add, [jnp.exp2(part - peak) for part in parts])
    return peak + jnp.log2(total)


def half_step(from_points, to_points, weights, parts, m_list, n_list, count, from_first, keep_total):
    m_blocks, width, _ = from_points.shape
    n_blocks = to_points.shape[0]
    dim = width // 2
    n_parts = len(parts)
    groups = TILE // 8

    def kernel(*refs):
        m_idx, n_idx, size, a_ref, b_ref = refs[:5]
        if n_parts:
            w_ref, part_refs = refs[5], refs[6 : 6 + n_parts]
            out_refs = refs[6 + n_parts :]
        else:
            w_ref, part_refs, out_refs = refs[5], (), refs[6:]
        out_ref = out_refs[0]
        scratch = out_refs[2:] if keep_total else out_refs[1:]
        bias, peaks, sums, s0, s1, p0, p1 = scratch

        if n_parts:
            total = log_sum([ref[...] for ref in part_refs])
            if keep_total:
                out_refs[1][...] = total
            lift = w_ref[...] - total
        else:
            lift = w_ref[...]
        high = lift.astype(jnp.bfloat16).astype(jnp.float32)
        rest = lift - high
        middle = rest.astype(jnp.bfloat16).astype(jnp.float32)
        low = rest - middle
        place = lax.broadcasted_iota(jnp.int32, (BIAS, TILE), 0)
        for i in range(m_blocks):
            rows = jnp.where(
                place == 0,
                high[i : i + 1, :],
                jnp.where(place == 1, middle[i : i + 1, :], jnp.where(place == 2, low[i : i + 1, :], 0.0)),
            )
            bias[i] = rows.astype(jnp.bfloat16)
        peaks[...] = jnp.full(peaks.shape, lowest, jnp.float32)
        sums[...] = jnp.zeros(sums.shape, jnp.float32)
        ones = jnp.where(place < 3, 1.0, 0.0).astype(jnp.bfloat16)
        n = size[0]

        def doubled(ref, i, high_first):
            both = ref[i]
            if high_first:
                return [both[0:dim], both]
            return [both, both[0:dim]]

        def scores(k, score, peak):
            k = jnp.minimum(k, n)
            m, c = m_idx[k], n_idx[k]
            left = jnp.concatenate(doubled(a_ref, m, not from_first) + [bias[m]], axis=0)
            right = jnp.concatenate(doubled(b_ref, c, from_first) + [ones], axis=0)
            value = lax.dot_general(left, right, (((0,), (0,)), ((), ())), preferred_element_type=jnp.float32)
            value = value.reshape(groups, 8, TILE)
            score[...] = value
            peak[...] = jnp.max(value, axis=0)

        def absorb(k, score, peak):
            c = jnp.where(k < n, n_idx[jnp.minimum(k, n)], n_blocks)
            before = peaks[c]
            after = jnp.maximum(before, peak[...])
            total = jnp.sum(jnp.exp2(score[...] - after[None]), axis=0)
            sums[c] = sums[c] * jnp.exp2(before - after) + total
            peaks[c] = after

        scores(0, s0, p0)

        def visit(step, carry):
            scores(2 * step + 1, s1, p1)
            absorb(2 * step, s0, p0)
            scores(2 * step + 2, s0, p0)
            absorb(2 * step + 1, s1, p1)
            return carry

        lax.fori_loop(0, lax.div(n + 1, 2), visit, 0)
        top = peaks[0:n_blocks]
        peak = jnp.max(top, axis=1)
        total = jnp.sum(sums[0:n_blocks] * jnp.exp2(top - peak[:, None, :]), axis=1)
        out_ref[...] = jnp.where(total > 0.0, peak + jnp.log2(total), lowest)

    f32 = jnp.float32
    shape = jax.ShapeDtypeStruct
    out_shape = [shape((n_blocks, TILE), f32)] + ([shape((m_blocks, TILE), f32)] if keep_total else [])
    return pl.pallas_call(
        kernel,
        out_shape=out_shape,
        in_specs=[SM] * 3 + [VM] * (3 + n_parts),
        out_specs=[VM] * len(out_shape),
        scratch_shapes=[
            pltpu.VMEM((m_blocks, BIAS, TILE), jnp.bfloat16),
            pltpu.VMEM((n_blocks + 1, 8, TILE), f32),
            pltpu.VMEM((n_blocks + 1, 8, TILE), f32),
            pltpu.VMEM((groups, 8, TILE), f32),
            pltpu.VMEM((groups, 8, TILE), f32),
            pltpu.VMEM((8, TILE), f32),
            pltpu.VMEM((8, TILE), f32),
        ],
        compiler_params=PARAMS,
        name="column_step" if from_first else "row_step",
    )(m_list, n_list, count, from_points, to_points, weights, *parts)


def per_device(samples, sample_logw, references, reference_logw, dual_start, kept_tiles, tile_counts):
    n_row, n_col = lax.axis_size("row"), lax.axis_size("col")
    dim = samples.shape[1]
    own_row_blocks = samples.shape[0] // TILE
    own_col_blocks = references.shape[0] // TILE
    row_blocks, col_blocks = own_row_blocks * n_col, own_col_blocks * n_row
    chunks = TILE // LANES
    parity = lax.axis_index("row") % 2
    both = own_col_blocks % 2 == 0
    assert both or own_col_blocks == 1

    shape = jax.ShapeDtypeStruct
    depth = chunks * (dim + 1)
    kept = own_col_blocks // 2 if both else own_col_blocks
    packed_shapes = [shape((own_row_blocks, depth, LANES), jnp.float32)]
    packed_shapes += [shape((kept, depth, LANES), jnp.float32)] * (2 if both else 1)
    packed = pl.pallas_call(
        pack_kernel,
        out_shape=packed_shapes,
        in_specs=[VM] * 4,
        out_specs=[VM] * len(packed_shapes),
        compiler_params=PARAMS,
        name="pack",
    )(
        samples.T,
        sample_logw.reshape(-1, LANES),
        references.T,
        reference_logw.reshape(-1, LANES),
    )
    x_pack, y_keep = packed[0], packed[1]
    own_y = [y_keep] + [swap(y_keep, "row", 2 * d) for d in range(1, n_row // 2)]
    partner_y = []
    if both:
        y_other = swap(packed[2], "row", 1)
        partner_y = [y_other] + [swap(y_other, "row", 2 * d) for d in range(1, n_row // 2)]
    own_x = [x_pack] + [swap(x_pack, "col", d) for d in range(1, n_col)]
    partner_x = [swap(part, "row", 1) for part in own_x]
    dual_partner = swap(dual_start, "row", 1)
    tiles_own = jnp.concatenate([kept_tiles[0, 0], tile_counts[0]])
    tiles_partner = swap(tiles_own, "row", 1)
    xp, yp, start, wx, wy, nx, ny, m_list, n_list, count = prepare(
        own_x, partner_x, own_y, partner_y, dual_start, dual_partner,
        tiles_own, tiles_partner, (row_blocks, col_blocks, dim),
    )

    row_parts = []
    for turn in range(ITERS):
        last = turn == ITERS - 1
        (part,) = half_step(xp, yp, wx if turn else start, row_parts, m_list, n_list, count, True, False)
        col_parts = [part] + [swap(part, "row", 2 * d) for d in range(1, n_row // 2)]
        part, *kept_total = half_step(yp, xp, wy, col_parts, n_list, m_list, count, False, last)
        part = log_sum([part, swap(part, "row", 1)])
        row_parts = [part] + [swap(part, "col", d) for d in range(1, n_col)]

    own = [lax.dynamic_slice_in_dim(part, parity * row_blocks, row_blocks, 0) for part in row_parts]
    norms = lax.dynamic_slice_in_dim(nx, parity * row_blocks, row_blocks, 0)
    row_duals = norms - (epsilon * ln2) * log_sum(own)
    col_half = ny - (epsilon * ln2) * kept_total[0]
    col_other = swap(col_half, "row", 1)
    even = jnp.where(parity == 0, col_half, col_other)
    odd = jnp.where(parity == 0, col_other, col_half)
    col_duals = jnp.stack([even, odd], axis=1)
    return (row_duals.reshape(1, -1), col_duals.reshape(1, -1))


def solution(mesh):
    return jax.shard_map(
        per_device,
        mesh=mesh,
        in_specs=(
            P(("row", "col"), None),
            P(("row", "col")),
            P(("row", "col"), None),
            P(("row", "col")),
            P("row", None),
            P("row", "col", None),
            P("row", "col"),
        ),
        out_specs=(P("row", None), P("col", None)),
        check_vma=False,
    )
```

time: 859 us -> 137 us (0.16)
  matrix products: 242 us -> 0 us
  local copies, waits for them, and re-layouts: 206 us -> 5.29 us
  blocking collectives: 175 us -> 0 us
  loops' own time: 151 us -> 0 us
  Pallas kernels: 0 us -> 54.5 us
  other arithmetic: 47.1 us -> 0.23 us
  starting transfers between devices: 3.19 us -> 42.6 us
  waiting for transfers between devices: 14.7 us -> 32.3 us
  between operations: 16.5 us -> 1.52 us
    dot_general x108 -> x0, matrix products: 242 us -> none  [tile_cost(): jnp.dot(row_points, col_points.T, precision=lax.Precision.HIGHEST, prefer...]
    all_gather x15 -> x0, blocking collectives: 175 us -> none  [the longest x12 135 us: merged_2(): pieces = jax.tree.map(lambda part: lax.all_gather(part, axis), value)]
    dynamic_slice x678 -> x0, local copies, waits for them, and re-layouts: 172 us -> none  [the longest x108 68.2 us: locate(): low_tiles[jnp.minimum(position, slots - 1)]]
    another operation x12 -> x0, loops' own time: 151 us -> none  [the longest x3 77.6 us: per_device(): row_peaks, row_sums = lax.fori_loop(0, work, row_visit, start_state)]
    pallas_call x0 -> x8, Pallas kernels: none -> 54.5 us  [the longest x6 52.1 us: half_step(): pl.pallas_call(kernel, out_shape=out_shape, in_specs=[SM] * 3 + [VM] * (3...]
    ppermute x13 -> x38, starting transfers between devices: 3.15 us -> 42.6 us  [swap(): return jax.tree.map(lambda part: lax.ppermute(part, axis, pairs), value)]
    dynamic_update_slice x108 -> x0, local copies, waits for them, and re-layouts: 27.8 us -> none  [the longest x54 13.9 us: row_visit(): lax.dynamic_update_slice(carry[1], merged[1][None], (source, row_start))]
    ppermute x13 -> x38, waiting for transfers between devices: 5.2 us -> 32.3 us  [swap(): return jax.tree.map(lambda part: lax.ppermute(part, axis, pairs), value)]
  transfers between devices with their start and end apart: 14 -> 38, of which waited for: 9 -> 23; matrix products, arithmetic and copies ran while one was open for 1% -> 1% of each run, Pallas kernels for 0% -> 0%
where the time goes in v1:
time: 137 us; the launch traced here: 136 us
  Pallas kernels  54.5 us (40%)
  starting transfers between devices  42.6 us (31%)
  waiting for transfers between devices  32.3 us (24%)
  local copies, waits for them, and re-layouts  5.29 us (4%)
  between operations  1.52 us (1%)
    pallas_call x6, Pallas kernels, half_step(): pl.pallas_call(kernel, out_shape=out_shape, in_specs=[SM] * 3 + [VM] * (3...  52.1 us
    ppermute x38, starting transfers between devices, swap(): return jax.tree.map(lambda part: lax.ppermute(part, axis, pairs), value)  42.6 us
    ppermute x38, waiting for transfers between devices, swap(): return jax.tree.map(lambda part: lax.ppermute(part, axis, pairs), value)  32.3 us
    unnamed x13, local copies, waits for them, and re-layouts  4.51 us
  transfers between devices with their start and end apart: 38, of which 23 were waited for; matrix products, arithmetic and copies ran while one was open for 1% of the time, Pallas kernels for 0%

profile of v1, /device:TPU:0, one launch (start us, length us, event | category | flops | bytes accessed | tf_op | source)
XLA Modules:
  0.0 136.4 jit_solution(18435522192424257380)
XLA Ops:
  3.9 3.1 %collective-permute-start = (f32[2,132,128]{2,1,0:T(8,128)S(1)}, f32[2,132,128]{2,1,0:T(8,128)S(1)}, u32[]{:S(2)}, u32[]{:S(2)}) collective-permute-start(f32[2,132,128]{2,1,0:T(8,128)S(1)} %get-tuple-element.17.refs_0_), channel_id=1, source_target_pairs={{0,1},{1,0},{2,3},{3,2},{4,5},{5,4},{6,7},{7,6},{8,9},{9,8},{10,11... | collective-permute-start | bytes 405512 | tf_op jit(solution)/shard_map/ppermute | solution.py:28
  7.0 2.6 %collective-permute-start.1 = (f32[2,132,128]{2,1,0:T(8,128)S(1)}, f32[2,132,128]{2,1,0:T(8,128)S(1)}, u32[]{:S(2)}, u32[]{:S(2)}) collective-permute-start(f32[2,132,128]{2,1,0:T(8,128)S(1)} %get-tuple-element.17.refs_0_), channel_id=1, source_target_pairs={{0,2},{1,3},{2,0},{3,1},{4,6},{5,7},{6,4},{7,5},{8,10},{9,11},{10,... | collective-permute-start | bytes 405512 | tf_op jit(solution)/shard_map/ppermute | solution.py:28
  13.9 1.7 %collective-permute-start.7 = (f32[2,132,128]{2,1,0:T(8,128)S(1)}, f32[2,132,128]{2,1,0:T(8,128)S(1)}, u32[]{:S(2)}, u32[]{:S(2)}) collective-permute-start(f32[2,132,128]{2,1,0:T(8,128)S(1)} %get-tuple-element.18.refs_8_), channel_id=1, source_target_pairs={{0,8},{4,12},{8,0},{12,4},{16,24},{20,28},{24,16},{28,20},{1,9},{5... | collective-permute-start | bytes 405512 | tf_op jit(solution)/shard_map/ppermute | solution.py:28
  15.6 4.9 %collective-permute-done.1.refs_2_ = f32[2,132,128]{2,1,0:T(8,128)S(1)} collective-permute-done((f32[2,132,128]{2,1,0:T(8,128)S(1)}, f32[2,132,128]{2,1,0:T(8,128)S(1)}, u32[]{:S(2)}, u32[]{:S(2)}) %collective-permute-start.1) | collective-permute-done | bytes 135200 | tf_op jit(solution)/shard_map/ppermute | solution.py:28
  28.5 3.2 %collective-permute-start.13 = (f32[2,132,128]{2,1,0:T(8,128)S(1)}, f32[2,132,128]{2,1,0:T(8,128)S(1)}, u32[]{:S(2)}, u32[]{:S(2)}) collective-permute-start(f32[2,132,128]{2,1,0:T(8,128)S(1)} %collective-permute-done.10.refs_12_), channel_id=1, source_target_pairs={{0,24},{4,28},{8,16},{12,20},{16,8},{20,12},{24,0},{28,4},{1,25},{... | collective-permute-start | bytes 405512 | tf_op jit(solution)/shard_map/ppermute | solution.py:28
  34.8 2.3 %prepare.1 = (bf16[16,64,512]{2,1,0:T(8,128)(2,1)S(1)}, bf16[16,64,512]{2,1,0:T(8,128)(2,1)S(1)}, f32[16,512]{1,0:T(8,128)S(1)}, f32[16,512]{1,0:T(8,128)S(1)}, ...) custom-call(f32[2,132,128]{2,1,0:T(8,128)S(1)} %get-tuple-element.17, ...), custom_call_target="tpu_custom_call" | custom-call | tf_op jit(solution)/shard_map/prepare/pallas_call | solution.py:146
  37.2 8.7 %column_step.3.refs_6_ = f32[16,512]{1,0:T(8,128)S(1)} custom-call(s32[66]{0:T(128)S(1)} %get-tuple-element.22.refs_0_.refs_1_, s32[66]{0:T(128)S(1)} %get-tuple-element.21.refs_1_.refs_0_, s32[1]{0:T(128)} %get-tuple-element.23.refs_2_, bf16[16,64,512]{2,1,0:T(8,128)(2,1)S(1)} %get-tuple-element.25.refs_3_.refs_4_, ...), custom_call_target="tpu_custom_call" | custom-call | tf_op jit(solution)/shard_map/column_step/pallas_call | solution.py:259
  45.9 2.1 %collective-permute-start.17 = (f32[16,512]{1,0:T(8,128)S(1)}, f32[16,512]{1,0:T(8,128)S(1)}, u32[]{:S(2)}, u32[]{:S(2)}) collective-permute-start(f32[16,512]{1,0:T(8,128)S(1)} %column_step.3.refs_6_), channel_id=1, source_target_pairs={{0,16},{4,20},{8,24},{12,28},{16,0},{20,4},{24,8},{28,12},{1,17},{... | collective-permute-start | bytes 98312 | tf_op jit(solution)/shard_map/ppermute | solution.py:28
  49.9 2.9 %collective-permute-done.18.refs_9_ = f32[16,512]{1,0:T(8,128)S(1)} collective-permute-done((f32[16,512]{1,0:T(8,128)S(1)}, f32[16,512]{1,0:T(8,128)S(1)}, u32[]{:S(2)}, u32[]{:S(2)}) %collective-permute-start.18) | collective-permute-done | bytes 32800 | tf_op jit(solution)/shard_map/ppermute | solution.py:28
  52.8 8.7 %row_step.3 = f32[16,512]{1,0:T(8,128)S(1)} custom-call(s32[66]{0:T(128)S(1)} %get-tuple-element.21.refs_1_.refs_0_, s32[66]{0:T(128)S(1)} %get-tuple-element.22.refs_0_.refs_1_, s32[1]{0:T(128)} %get-tuple-element.23.refs_2_, bf16[16,64,512]{2,1,0:T(8,128)(2,1)S(1)} %get-tuple-element.24.refs_4_.refs_3_, ...), custom_call_target="tpu_custom_call" | custom-call | tf_op jit(solution)/shard_map/row_step/pallas_call | solution.py:259
  62.9 2.0 %collective-permute-start.21 = (f32[16,512]{1,0:T(8,128)S(1)}, f32[16,512]{1,0:T(8,128)S(1)}, u32[]{:S(2)}, u32[]{:S(2)}) collective-permute-start(f32[16,512]{1,0:T(8,128)S(1)} %multiply_add_fusion.2.refs_6_), channel_id=1, source_target_pairs={{0,2},{1,3},{2,0},{3,1},{4,6},{5,7},{6,4},{7,5},{8,10},{9,11},{10,... | collective-permute-start | bytes 98312 | tf_op jit(solution)/shard_map/ppermute | solution.py:28
  64.9 2.3 %collective-permute-start.22 = (f32[16,512]{1,0:T(8,128)S(1)}, f32[16,512]{1,0:T(8,128)S(1)}, u32[]{:S(2)}, u32[]{:S(2)}) collective-permute-start(f32[16,512]{1,0:T(8,128)S(1)} %multiply_add_fusion.2.refs_6_), channel_id=1, source_target_pairs={{0,3},{1,2},{2,1},{3,0},{4,7},{5,6},{6,5},{7,4},{8,11},{9,10},{10,... | collective-permute-start | bytes 98312 | tf_op jit(solution)/shard_map/ppermute | solution.py:28
  68.2 2.4 %collective-permute-done.22.refs_9_ = f32[16,512]{1,0:T(8,128)S(1)} collective-permute-done((f32[16,512]{1,0:T(8,128)S(1)}, f32[16,512]{1,0:T(8,128)S(1)}, u32[]{:S(2)}, u32[]{:S(2)}) %collective-permute-start.22) | collective-permute-done | bytes 32800 | tf_op jit(solution)/shard_map/ppermute | solution.py:28
  70.6 8.7 %column_step.4.refs_6_ = f32[16,512]{1,0:T(8,128)S(1)} custom-call(s32[66]{0:T(128)S(1)} %get-tuple-element.22.refs_0_.refs_1_, s32[66]{0:T(128)S(1)} %get-tuple-element.21.refs_1_.refs_0_, s32[1]{0:T(128)} %get-tuple-element.23.refs_2_, bf16[16,64,512]{2,1,0:T(8,128)(2,1)S(1)} %get-tuple-element.25.refs_3_.refs_4_, ...), custom_call_target="tpu_custom_call" | custom-call | tf_op jit(solution)/shard_map/column_step/pallas_call | solution.py:259
  79.4 2.6 %collective-permute-start.24 = (f32[16,512]{1,0:T(8,128)S(1)}, f32[16,512]{1,0:T(8,128)S(1)}, u32[]{:S(2)}, u32[]{:S(2)}) collective-permute-start(f32[16,512]{1,0:T(8,128)S(1)} %column_step.4.refs_6_), channel_id=1, source_target_pairs={{0,16},{4,20},{8,24},{12,28},{16,0},{20,4},{24,8},{28,12},{1,17},{... | collective-permute-start | bytes 98312 | tf_op jit(solution)/shard_map/ppermute | solution.py:28
  83.9 2.9 %collective-permute-done.25.refs_9_ = f32[16,512]{1,0:T(8,128)S(1)} collective-permute-done((f32[16,512]{1,0:T(8,128)S(1)}, f32[16,512]{1,0:T(8,128)S(1)}, u32[]{:S(2)}, u32[]{:S(2)}) %collective-permute-start.25) | collective-permute-done | bytes 32800 | tf_op jit(solution)/shard_map/ppermute | solution.py:28
  86.8 8.7 %row_step.4 = f32[16,512]{1,0:T(8,128)S(1)} custom-call(s32[66]{0:T(128)S(1)} %get-tuple-element.21.refs_1_.refs_0_, s32[66]{0:T(128)S(1)} %get-tuple-element.22.refs_0_.refs_1_, s32[1]{0:T(128)} %get-tuple-element.23.refs_2_, bf16[16,64,512]{2,1,0:T(8,128)(2,1)S(1)} %get-tuple-element.24.refs_4_.refs_3_, ...), custom_call_target="tpu_custom_call" | custom-call | tf_op jit(solution)/shard_map/row_step/pallas_call | solution.py:259
  97.0 4.3 %collective-permute-start.29 = (f32[16,512]{1,0:T(8,128)S(1)}, f32[16,512]{1,0:T(8,128)S(1)}, u32[]{:S(2)}, u32[]{:S(2)}) collective-permute-start(f32[16,512]{1,0:T(8,128)S(1)} %multiply_add_fusion.1.refs_6_), channel_id=1, source_target_pairs={{0,3},{1,2},{2,1},{3,0},{4,7},{5,6},{6,5},{7,4},{8,11},{9,10},{10,... | collective-permute-start | bytes 98312 | tf_op jit(solution)/shard_map/ppermute | solution.py:28
  101.8 1.7 %collective-permute-done.29.refs_9_ = f32[16,512]{1,0:T(8,128)S(1)} collective-permute-done((f32[16,512]{1,0:T(8,128)S(1)}, f32[16,512]{1,0:T(8,128)S(1)}, u32[]{:S(2)}, u32[]{:S(2)}) %collective-permute-start.29) | collective-permute-done | bytes 32800 | tf_op jit(solution)/shard_map/ppermute | solution.py:28
  103.5 8.7 %column_step.5.refs_6_ = f32[16,512]{1,0:T(8,128)S(1)} custom-call(s32[66]{0:T(128)S(1)} %get-tuple-element.22.refs_0_.refs_1_, s32[66]{0:T(128)S(1)} %get-tuple-element.21.refs_1_.refs_0_, s32[1]{0:T(128)} %get-tuple-element.23.refs_2_, bf16[16,64,512]{2,1,0:T(8,128)(2,1)S(1)} %get-tuple-element.25.refs_3_.refs_4_, ...), custom_call_target="tpu_custom_call" | custom-call | tf_op jit(solution)/shard_map/column_step/pallas_call | solution.py:259
  112.3 1.9 %collective-permute-start.31 = (f32[16,512]{1,0:T(8,128)S(1)}, f32[16,512]{1,0:T(8,128)S(1)}, u32[]{:S(2)}, u32[]{:S(2)}) collective-permute-start(f32[16,512]{1,0:T(8,128)S(1)} %column_step.5.refs_6_), channel_id=1, source_target_pairs={{0,16},{4,20},{8,24},{12,28},{16,0},{20,4},{24,8},{28,12},{1,17},{... | collective-permute-start | bytes 98312 | tf_op jit(solution)/shard_map/ppermute | solution.py:28
  116.3 2.8 %collective-permute-done.32.refs_9_ = f32[16,512]{1,0:T(8,128)S(1)} collective-permute-done((f32[16,512]{1,0:T(8,128)S(1)}, f32[16,512]{1,0:T(8,128)S(1)}, u32[]{:S(2)}, u32[]{:S(2)}) %collective-permute-start.32) | collective-permute-done | bytes 32800 | tf_op jit(solution)/shard_map/ppermute | solution.py:28
  119.1 8.7 %row_step.5 = (f32[16,512]{1,0:T(8,128)S(1)}, f32[16,512]{1,0:T(8,128)S(1)}) custom-call(s32[66]{0:T(128)S(1)} %get-tuple-element.21.refs_1_.refs_0_, s32[66]{0:T(128)S(1)} %get-tuple-element.22.refs_0_.refs_1_, s32[1]{0:T(128)} %get-tuple-element.23.refs_2_, bf16[16,64,512]{2,1,0:T(8,128)(2,1)S(1)} %get-tuple-element.24.refs_4_.refs_3_, ...), custom_call_target="tpu_custom_call" | custom-call | tf_op jit(solution)/shard_map/row_step/pallas_call | solution.py:259
  129.8 3.7 %collective-permute-start.36 = (f32[16,512]{1,0:T(8,128)S(1)}, f32[16,512]{1,0:T(8,128)S(1)}, u32[]{:S(2)}, u32[]{:S(2)}) collective-permute-start(f32[16,512]{1,0:T(8,128)S(1)} %multiply_add_fusion), channel_id=1, source_target_pairs={{0,3},{1,2},{2,1},{3,0},{4,7},{5,6},{6,5},{7,4},{8,11},{9,10},{10,... | collective-permute-start | bytes 98312 | tf_op jit(solution)/shard_map/ppermute | solution.py:28
  (83 shorter events, 33.2 us)
Async XLA Ops:
  3.9 10.0 %collective-permute-start = (f32[2,132,128]{2,1,0:T(8,128)S(1)}, f32[2,132,128]{2,1,0:T(8,128)S(1)}, u32[]{:S(2)}, u32[]{:S(2)}) collective-permute-start(f32[2,132,128]{2,1,0:T(8,128)S(1)} %get-tuple-element.17.refs_0_), channel_id=1, source_target_pairs={{0,1},{1,0},{2,3},{3,2},{4,5},{5,4},{6,7},{7,6},{8,9},{9,8},{10,11... | collective-permute-start | bytes 405512 | tf_op jit(solution)/shard_map/ppermute | solution.py:28
  7.0 13.4 %collective-permute-start.1 = (f32[2,132,128]{2,1,0:T(8,128)S(1)}, f32[2,132,128]{2,1,0:T(8,128)S(1)}, u32[]{:S(2)}, u32[]{:S(2)}) collective-permute-start(f32[2,132,128]{2,1,0:T(8,128)S(1)} %get-tuple-element.17.refs_0_), channel_id=1, source_target_pairs={{0,2},{1,3},{2,0},{3,1},{4,6},{5,7},{6,4},{7,5},{8,10},{9,11},{10,... | collective-permute-start | bytes 405512 | tf_op jit(solution)/shard_map/ppermute | solution.py:28
  9.6 12.3 %collective-permute-start.2 = (f32[2,132,128]{2,1,0:T(8,128)S(1)}, f32[2,132,128]{2,1,0:T(8,128)S(1)}, u32[]{:S(2)}, u32[]{:S(2)}) collective-permute-start(f32[2,132,128]{2,1,0:T(8,128)S(1)} %get-tuple-element.17.refs_0_), channel_id=1, source_target_pairs={{0,3},{1,2},{2,1},{3,0},{4,7},{5,6},{6,5},{7,4},{8,11},{9,10},{10,... | collective-permute-start | bytes 405512 | tf_op jit(solution)/shard_map/ppermute | solution.py:28
  9.6 13.8 %collective-permute-start.3 = (f32[2,132,128]{2,1,0:T(8,128)S(1)}, f32[2,132,128]{2,1,0:T(8,128)S(1)}, u32[]{:S(2)}, u32[]{:S(2)}) collective-permute-start(f32[2,132,128]{2,1,0:T(8,128)S(1)} %get-tuple-element.17.refs_0_), channel_id=1, source_target_pairs={{0,4},{4,0},{8,12},{12,8},{16,20},{20,16},{24,28},{28,24},{1,5},{5... | collective-permute-start | bytes 405512 | tf_op jit(solution)/shard_map/ppermute | solution.py:28
  13.5 9.9 %collective-permute-start.10 = (f32[2,132,128]{2,1,0:T(8,128)S(1)}, f32[2,132,128]{2,1,0:T(8,128)S(1)}, u32[]{:S(2)}, u32[]{:S(2)}) collective-permute-start(f32[2,132,128]{2,1,0:T(8,128)S(1)} %get-tuple-element.19), channel_id=1, source_target_pairs={{0,4},{4,0},{8,12},{12,8},{16,20},{20,16},{24,28},{28,24},{1,5},{5... | collective-permute-start | bytes 405512 | tf_op jit(solution)/shard_map/ppermute | solution.py:28
  13.9 10.1 %collective-permute-start.7 = (f32[2,132,128]{2,1,0:T(8,128)S(1)}, f32[2,132,128]{2,1,0:T(8,128)S(1)}, u32[]{:S(2)}, u32[]{:S(2)}) collective-permute-start(f32[2,132,128]{2,1,0:T(8,128)S(1)} %get-tuple-element.18.refs_8_), channel_id=1, source_target_pairs={{0,8},{4,12},{8,0},{12,4},{16,24},{20,28},{24,16},{28,20},{1,9},{5... | collective-permute-start | bytes 405512 | tf_op jit(solution)/shard_map/ppermute | solution.py:28
  20.5 5.1 %collective-permute-start.8 = (f32[2,132,128]{2,1,0:T(8,128)S(1)}, f32[2,132,128]{2,1,0:T(8,128)S(1)}, u32[]{:S(2)}, u32[]{:S(2)}) collective-permute-start(f32[2,132,128]{2,1,0:T(8,128)S(1)} %get-tuple-element.18.refs_8_), channel_id=1, source_target_pairs={{0,16},{4,20},{8,24},{12,28},{16,0},{20,4},{24,8},{28,12},{1,17},{... | collective-permute-start | bytes 405512 | tf_op jit(solution)/shard_map/ppermute | solution.py:28
  22.0 6.0 %collective-permute-start.9 = (f32[2,132,128]{2,1,0:T(8,128)S(1)}, f32[2,132,128]{2,1,0:T(8,128)S(1)}, u32[]{:S(2)}, u32[]{:S(2)}) collective-permute-start(f32[2,132,128]{2,1,0:T(8,128)S(1)} %get-tuple-element.18.refs_8_), channel_id=1, source_target_pairs={{0,24},{4,28},{8,16},{12,20},{16,8},{20,12},{24,0},{28,4},{1,25},{... | collective-permute-start | bytes 405512 | tf_op jit(solution)/shard_map/ppermute | solution.py:28
  23.4 5.1 %collective-permute-start.4 = (f32[2,132,128]{2,1,0:T(8,128)S(1)}, f32[2,132,128]{2,1,0:T(8,128)S(1)}, u32[]{:S(2)}, u32[]{:S(2)}) collective-permute-start(f32[2,132,128]{2,1,0:T(8,128)S(1)} %collective-permute-done.refs_1_), channel_id=1, source_target_pairs={{0,4},{4,0},{8,12},{12,8},{16,20},{20,16},{24,28},{28,24},{1,5},{5... | collective-permute-start | bytes 405512 | tf_op jit(solution)/shard_map/ppermute | solution.py:28
  23.4 8.4 %collective-permute-start.5 = (f32[2,132,128]{2,1,0:T(8,128)S(1)}, f32[2,132,128]{2,1,0:T(8,128)S(1)}, u32[]{:S(2)}, u32[]{:S(2)}) collective-permute-start(f32[2,132,128]{2,1,0:T(8,128)S(1)} %collective-permute-done.1.refs_2_), channel_id=1, source_target_pairs={{0,4},{4,0},{8,12},{12,8},{16,20},{20,16},{24,28},{28,24},{1,5},{5... | collective-permute-start | bytes 405512 | tf_op jit(solution)/shard_map/ppermute | solution.py:28
  23.9 7.9 %collective-permute-start.6 = (f32[2,132,128]{2,1,0:T(8,128)S(1)}, f32[2,132,128]{2,1,0:T(8,128)S(1)}, u32[]{:S(2)}, u32[]{:S(2)}) collective-permute-start(f32[2,132,128]{2,1,0:T(8,128)S(1)} %collective-permute-done.2.refs_3_), channel_id=1, source_target_pairs={{0,4},{4,0},{8,12},{12,8},{16,20},{20,16},{24,28},{28,24},{1,5},{5... | collective-permute-start | bytes 405512 | tf_op jit(solution)/shard_map/ppermute | solution.py:28
  25.5 6.3 %collective-permute-start.11 = (f32[2,132,128]{2,1,0:T(8,128)S(1)}, f32[2,132,128]{2,1,0:T(8,128)S(1)}, u32[]{:S(2)}, u32[]{:S(2)}) collective-permute-start(f32[2,132,128]{2,1,0:T(8,128)S(1)} %collective-permute-done.10.refs_12_), channel_id=1, source_target_pairs={{0,8},{4,12},{8,0},{12,4},{16,24},{20,28},{24,16},{28,20},{1,9},{5... | collective-permute-start | bytes 405512 | tf_op jit(solution)/shard_map/ppermute | solution.py:28
  28.0 5.2 %collective-permute-start.12 = (f32[2,132,128]{2,1,0:T(8,128)S(1)}, f32[2,132,128]{2,1,0:T(8,128)S(1)}, u32[]{:S(2)}, u32[]{:S(2)}) collective-permute-start(f32[2,132,128]{2,1,0:T(8,128)S(1)} %collective-permute-done.10.refs_12_), channel_id=1, source_target_pairs={{0,16},{4,20},{8,24},{12,28},{16,0},{20,4},{24,8},{28,12},{1,17},{... | collective-permute-start | bytes 405512 | tf_op jit(solution)/shard_map/ppermute | solution.py:28
  28.5 6.3 %collective-permute-start.13 = (f32[2,132,128]{2,1,0:T(8,128)S(1)}, f32[2,132,128]{2,1,0:T(8,128)S(1)}, u32[]{:S(2)}, u32[]{:S(2)}) collective-permute-start(f32[2,132,128]{2,1,0:T(8,128)S(1)} %collective-permute-done.10.refs_12_), channel_id=1, source_target_pairs={{0,24},{4,28},{8,16},{12,20},{16,8},{20,12},{24,0},{28,4},{1,25},{... | collective-permute-start | bytes 405512 | tf_op jit(solution)/shard_map/ppermute | solution.py:28
  48.0 4.8 %collective-permute-start.18 = (f32[16,512]{1,0:T(8,128)S(1)}, f32[16,512]{1,0:T(8,128)S(1)}, u32[]{:S(2)}, u32[]{:S(2)}) collective-permute-start(f32[16,512]{1,0:T(8,128)S(1)} %column_step.3.refs_6_), channel_id=1, source_target_pairs={{0,24},{4,28},{8,16},{12,20},{16,8},{20,12},{24,0},{28,4},{1,25},{... | collective-permute-start | bytes 98312 | tf_op jit(solution)/shard_map/ppermute | solution.py:28
  62.9 5.3 %collective-permute-start.21 = (f32[16,512]{1,0:T(8,128)S(1)}, f32[16,512]{1,0:T(8,128)S(1)}, u32[]{:S(2)}, u32[]{:S(2)}) collective-permute-start(f32[16,512]{1,0:T(8,128)S(1)} %multiply_add_fusion.2.refs_6_), channel_id=1, source_target_pairs={{0,2},{1,3},{2,0},{3,1},{4,6},{5,7},{6,4},{7,5},{8,10},{9,11},{10,... | collective-permute-start | bytes 98312 | tf_op jit(solution)/shard_map/ppermute | solution.py:28
  64.9 5.7 %collective-permute-start.22 = (f32[16,512]{1,0:T(8,128)S(1)}, f32[16,512]{1,0:T(8,128)S(1)}, u32[]{:S(2)}, u32[]{:S(2)}) collective-permute-start(f32[16,512]{1,0:T(8,128)S(1)} %multiply_add_fusion.2.refs_6_), channel_id=1, source_target_pairs={{0,3},{1,2},{2,1},{3,0},{4,7},{5,6},{6,5},{7,4},{8,11},{9,10},{10,... | collective-permute-start | bytes 98312 | tf_op jit(solution)/shard_map/ppermute | solution.py:28
  82.0 4.8 %collective-permute-start.25 = (f32[16,512]{1,0:T(8,128)S(1)}, f32[16,512]{1,0:T(8,128)S(1)}, u32[]{:S(2)}, u32[]{:S(2)}) collective-permute-start(f32[16,512]{1,0:T(8,128)S(1)} %column_step.4.refs_6_), channel_id=1, source_target_pairs={{0,24},{4,28},{8,16},{12,20},{16,8},{20,12},{24,0},{28,4},{1,25},{... | collective-permute-start | bytes 98312 | tf_op jit(solution)/shard_map/ppermute | solution.py:28
  96.9 4.9 %collective-permute-start.28 = (f32[16,512]{1,0:T(8,128)S(1)}, f32[16,512]{1,0:T(8,128)S(1)}, u32[]{:S(2)}, u32[]{:S(2)}) collective-permute-start(f32[16,512]{1,0:T(8,128)S(1)} %multiply_add_fusion.1.refs_6_), channel_id=1, source_target_pairs={{0,2},{1,3},{2,0},{3,1},{4,6},{5,7},{6,4},{7,5},{8,10},{9,11},{10,... | collective-permute-start | bytes 98312 | tf_op jit(solution)/shard_map/ppermute | solution.py:28
  97.0 6.5 %collective-permute-start.29 = (f32[16,512]{1,0:T(8,128)S(1)}, f32[16,512]{1,0:T(8,128)S(1)}, u32[]{:S(2)}, u32[]{:S(2)}) collective-permute-start(f32[16,512]{1,0:T(8,128)S(1)} %multiply_add_fusion.1.refs_6_), channel_id=1, source_target_pairs={{0,3},{1,2},{2,1},{3,0},{4,7},{5,6},{6,5},{7,4},{8,11},{9,10},{10,... | collective-permute-start | bytes 98312 | tf_op jit(solution)/shard_map/ppermute | solution.py:28
  127.9 5.7 %collective-permute-start.37 = (f32[16,512]{1,0:T(8,128)S(1)}, f32[16,512]{1,0:T(8,128)S(1)}, u32[]{:S(2)}, u32[]{:S(2)}) collective-permute-start(f32[16,512]{1,0:T(8,128)S(1)} %multiply_subtract_fusion), channel_id=1, source_target_pairs={{0,4},{4,0},{8,12},{12,8},{16,20},{20,16},{24,28},{28,24},{1,5},{5... | collective-permute-start | bytes 98312 | tf_op jit(solution)/shard_map/ppermute | solution.py:28
  129.1 5.3 %collective-permute-start.34 = (f32[16,512]{1,0:T(8,128)S(1)}, f32[16,512]{1,0:T(8,128)S(1)}, u32[]{:S(2)}, u32[]{:S(2)}) collective-permute-start(f32[16,512]{1,0:T(8,128)S(1)} %multiply_add_fusion), channel_id=1, source_target_pairs={{0,1},{1,0},{2,3},{3,2},{4,5},{5,4},{6,7},{7,6},{8,9},{9,8},{10,11... | collective-permute-start | bytes 98312 | tf_op jit(solution)/shard_map/ppermute | solution.py:28
  129.1 5.2 %collective-permute-start.35 = (f32[16,512]{1,0:T(8,128)S(1)}, f32[16,512]{1,0:T(8,128)S(1)}, u32[]{:S(2)}, u32[]{:S(2)}) collective-permute-start(f32[16,512]{1,0:T(8,128)S(1)} %multiply_add_fusion), channel_id=1, source_target_pairs={{0,2},{1,3},{2,0},{3,1},{4,6},{5,7},{6,4},{7,5},{8,10},{9,11},{10,... | collective-permute-start | bytes 98312 | tf_op jit(solution)/shard_map/ppermute | solution.py:28
  129.8 5.9 %collective-permute-start.36 = (f32[16,512]{1,0:T(8,128)S(1)}, f32[16,512]{1,0:T(8,128)S(1)}, u32[]{:S(2)}, u32[]{:S(2)}) collective-permute-start(f32[16,512]{1,0:T(8,128)S(1)} %multiply_add_fusion), channel_id=1, source_target_pairs={{0,3},{1,2},{2,1},{3,0},{4,7},{5,6},{6,5},{7,4},{8,11},{9,10},{10,... | collective-permute-start | bytes 98312 | tf_op jit(solution)/shard_map/ppermute | solution.py:28
  (20 other events, 57.0 us)
